TPU v7x, 512 devices: a whole 4x8x8 slice. The times are simulated.
512 devices in a mesh: lat: 64 (over y, z), ma: 8 (over x, core).
Axes of the slice: x: 4, y: 8, z: 8, core: 2. Of those that a mesh axis runs over, the one named last changes fastest.
Arguments:
- pair_wave: int32 [360], replicated, may hold values from 0 to 359, each once
- legendre: bfloat16 [360, 640, 768], P('ma', 'lat'), may hold values from -0.0078125 to 0.0078125
- coefs: bfloat16 [360, 768, 168], P('ma', 'lat'), may hold values from -6 to 6
Outputs:
- noise: float32 [53760, 1440], P(('lat', 'ma'))
Inputs may be any that keep to these rules, and one draw needn't show every extreme that they name: Slot q holds wavenumbers pair_wave[q] and 719 - pair_wave[q]; every value appears once.
All inputs are finite; a program needn't handle non-finite values.
Results may differ from a plain program's by a relative error of at most 0.0003.
Values may be sent and summed in bfloat16 or wider, within the bound.
A program may use at most 64 MiB of HBM per device.

v0:
```python
import math

import jax
import jax.numpy as jnp
from jax import lax
from jax.sharding import Mesh
from jax.sharding import PartitionSpec as P

DEG = 720
LON = 1440
CH = 84
LAT_DEV = 10
MA = ("ma_0", "ma_1")
LAT_MA = ("lat", "ma_0", "ma_1")


def split_up(shard, dim, count):
    before, after = (shard.shape[:dim], shard.shape[dim + 1 :])
    return jnp.moveaxis(shard.reshape(*before, count, -1, *after), dim, 0)


def in_order(pieces, dim):
    pieces = jnp.moveaxis(pieces, 0, dim)
    dims = pieces.shape
    return pieces.reshape(*dims[:dim], dims[dim] * dims[dim + 1], *dims[dim + 2 :])


def moved_by_axis(pieces, axes, turns):
    dims = [lax.axis_size(a) for a in axes]
    pieces = pieces.reshape(*dims, *pieces.shape[1:])
    for k in turns:
        pieces = lax.all_to_all(pieces, axes[k], split_axis=k, concat_axis=k, tiled=True)
    return pieces.reshape(-1, *pieces.shape[len(axes) :])


def exchange_by_axis(shard, axes, turns, split_dim, concat_dim):
    pieces = split_up(shard, split_dim, lax.axis_size(axes))
    return in_order(moved_by_axis(pieces, axes, turns), concat_dim)


def chain_table(table, wave_ids, degree_top):
    row_count = table.shape[2]
    row_ids = jnp.arange(row_count, dtype=jnp.int32)[None, :]
    split_row = (degree_top - wave_ids)[:, None]
    inside = row_ids < split_row
    outside = (row_ids >= split_row) & (row_ids <= degree_top)
    masks = jnp.stack([inside, outside], axis=1)
    return jnp.where(masks[:, :, None, :], table[:, None, :, :], jnp.zeros((), table.dtype))


def fourier_basis(pair_wave, degree_top, lon_count):
    orders = jnp.stack([pair_wave, degree_top - 1 - pair_wave], axis=1)
    positions = jnp.arange(lon_count, dtype=jnp.int32)
    phase_int = orders[:, :, None] * positions[None, None, :] % lon_count
    radians = 2.0 * math.pi / lon_count * phase_int.astype(jnp.float32)
    weight = jnp.where(orders == 0, 1.0, 2.0).astype(jnp.float32)[:, :, None]
    real_row = weight * jnp.cos(radians)
    imag_row = -weight * jnp.sin(radians)
    return jnp.stack([real_row, imag_row], axis=2).reshape(-1, lon_count)


def body(pair_wave, legendre, coefs):
    lat_count = lax.axis_size("lat")
    lat_place = lax.axis_index("lat")
    ma_place = lax.axis_index(MA)
    slot_count = coefs.shape[0]
    wave_ids = lax.dynamic_slice_in_dim(pair_wave, ma_place * slot_count, slot_count)
    per_device = (slot_count + lat_count - 1) // lat_count
    extra = per_device * lat_count - slot_count
    table_pad = jnp.concatenate(
        [legendre, jnp.zeros((extra,) + legendre.shape[1:], legendre.dtype)], axis=0
    )
    coefs_pad = jnp.concatenate([coefs, jnp.zeros((extra,) + coefs.shape[1:], coefs.dtype)], axis=0)
    waves_pad = jnp.concatenate([wave_ids, jnp.zeros((extra,), jnp.int32)], axis=0)
    tables_in, coefs_in = (
        lax.all_to_all(table_pad, "lat", split_axis=0, concat_axis=1, tiled=True),
        lax.all_to_all(coefs_pad, "lat", split_axis=0, concat_axis=1, tiled=True),
    )
    my_waves = lax.dynamic_slice_in_dim(waves_pad, lat_place * per_device, per_device)
    masked = chain_table(tables_in, my_waves, DEG)
    sums = jnp.einsum("qeir,qrc->qeic", masked, coefs_in, preferred_element_type=jnp.float32)
    returned = lax.all_to_all(sums, "lat", split_axis=2, concat_axis=0, tiled=True)
    spectra = returned[:slot_count]
    arranged = jnp.transpose(
        spectra.reshape(slot_count, 2, LAT_DEV, 2, CH), (0, 1, 3, 2, 4)
    ).reshape(slot_count, 2, 2, LAT_DEV * CH)
    exchanged = exchange_by_axis(arranged, MA, (1, 0), 3, 0)
    fourier_rows = exchanged.reshape(-1, exchanged.shape[3])
    synth_basis = fourier_basis(pair_wave, DEG, LON)
    return lax.dot_general(
        fourier_rows, synth_basis, (((0,), (0,)), ((), ())), precision=lax.Precision.HIGHEST
    )


def solution(mesh):
    split = Mesh(mesh.devices.reshape(mesh.shape["lat"], 4, 2), ("lat", "ma_0", "ma_1"))
    placed = (P(), P(MA, "lat", None), P(MA, "lat", None))
    return jax.shard_map(
        body, mesh=split, in_specs=placed, out_specs=P(LAT_MA, None), check_vma=False
    )
```

profile of v0, /device:TPU:1, one launch (start us, length us, event | category | flops | bytes accessed | tf_op | source)
XLA Modules:
  0.0 170.7 jit_solution(15079287082618436240)
XLA Ops:
  0.0 1.1 copy.42
  1.1 1.3 reshape.144
  2.4 17.1 %all-to-all-start.1 = ((bf16[64,2,1008]{2,1,0:T(2,128)(2,1)}), bf16[64,2,1008]{2,1,0:T(2,128)(2,1)S(1)}, u32[]{:S(2)}, u32[]{:S(2)}) async-start(bf16[64,2,1008]{2,1,0:T(2,128)(2,1)} %reshape.144), calls=%async_computation.1 | async-start | bytes 524288 | tf_op jit(solution)/shard_map/all_to_all | solution.py:77
  19.6 1.4 copy.41
  20.9 1.3 concatenate.17
  22.2 10.2 %all-to-all-done.1 = bf16[64,2,1008]{2,1,0:T(2,128)(2,1)S(1)} async-done(((bf16[64,2,1008]{2,1,0:T(2,128)(2,1)}), bf16[64,2,1008]{2,1,0:T(2,128)(2,1)S(1)}, u32[]{:S(2)}, u32[]{:S(2)}) %all-to-all-start.1) | async-done | bytes 258080 | tf_op jit(solution)/shard_map/all_to_all | solution.py:77
  32.4 5.6 %all-to-all-start = ((bf16[64,10,768]{2,1,0:T(8,128)(2,1)}), bf16[64,10,768]{2,1,0:T(8,128)(2,1)S(1)}, u32[]{:S(2)}, u32[]{:S(2)}) async-start(bf16[64,10,768]{2,1,0:T(8,128)(2,1)} %concatenate.17), calls=%async_computation | async-start | bytes 3145728 | tf_op jit(solution)/shard_map/all_to_all | solution.py:76
  38.7 0.7 compare_and_fusion
  39.4 0.7 reshape.145
  40.3 34.3 %all-to-all-done = bf16[64,10,768]{2,1,0:T(8,128)(2,1)S(1)} async-done(((bf16[64,10,768]{2,1,0:T(8,128)(2,1)}), bf16[64,10,768]{2,1,0:T(8,128)(2,1)S(1)}, u32[]{:S(2)}, u32[]{:S(2)}) %all-to-all-start) | async-done | bytes 983072 | tf_op jit(solution)/shard_map/all_to_all | solution.py:76
  75.0 0.8 fusion.8
  75.8 2.0 %copy.44 = f32[1,2,640,168]{3,1,0,2:T(2,128)} copy(f32[1,2,640,168]{2,3,1,0:T(8,128)S(1)} %fusion.8) | data formatting | bytes 1720320 | tf_op jit(solution)/shard_map/qeir,qrc->qeic/dot_general | solution.py:81
  77.9 10.3 %all-to-all-start.2 = ((f32[1,2,640,168]{3,1,0,2:T(2,128)}), f32[1,2,640,168]{3,1,0,2:T(2,128)S(1)}, u32[]{:S(2)}, u32[]{:S(2)}) async-start(f32[1,2,640,168]{3,1,0,2:T(2,128)} %copy.44), calls=%async_computation.2 | async-start | bytes 2621440 | tf_op jit(solution)/shard_map/all_to_all | solution.py:82
  88.3 21.3 %cosine_multiply_fusion = (f32[360,2,1,1440]{3,0,2,1:T(8,128)}, f32[360,2,1,1440]{3,0,2,1:T(8,128)}) fusion(s32[360,2]{0,1:T(2,128)S(1)} %pad_add_fusion, f32[360,2]{0,1:T(2,128)S(1)} %get-tuple-element.7, f32[360,2]{0,1:T(2,128)S(1)} %get-tuple-element.8), kind=kLoop, calls=%fused_computation.5 | loop fusion | flops 11404800 | bytes 8303040 | tf_op jit(solution)/shard_map/mul | solution.py:57
  109.6 9.3 %all-to-all-done.2 = f32[1,2,640,168]{3,1,0,2:T(2,128)S(1)} async-done(((f32[1,2,640,168]{3,1,0,2:T(2,128)}), f32[1,2,640,168]{3,1,0,2:T(2,128)S(1)}, u32[]{:S(2)}, u32[]{:S(2)}) %all-to-all-start.2) | async-done | bytes 860192 | tf_op jit(solution)/shard_map/all_to_all | solution.py:82
  119.2 1.2 reshape.140
  120.6 0.6 reshape_reshape.3
  121.6 9.1 %all_to_all.43 = f32[4,2,45,2,2,105]{5,4,3,2,0,1:T(2,128)S(1)} all-to-all(f32[4,2,45,2,2,105]{5,4,3,2,0,1:T(2,128)S(1)} %copy.46), channel_id=1, replica_groups=mesh['lat'=64,'ma_0'=4,'ma_1'=2] {'ma_1'}, dimensions={1} | all-to-all | bytes 1209600 | tf_op jit(solution)/shard_map/all_to_all | solution.py:32
  130.7 1.2 copy.47
  131.9 4.0 %all-to-all-start.4 = ((f32[4,2,45,2,2,105]{5,4,3,2,1,0:T(2,128)}), f32[4,2,45,2,2,105]{5,4,3,2,1,0:T(2,128)S(1)}, u32[]{:S(2)}, u32[]{:S(2)}) async-start(f32[4,2,45,2,2,105]{5,4,3,2,1,0:T(2,128)} %copy.47), calls=%async_computation.4 | async-start | bytes 1474560 | tf_op jit(solution)/shard_map/all_to_all | solution.py:32
  135.9 4.4 %pad_maximum_fusion = f32[360,2,2,1440]{3,0,2,1:T(8,128)S(1)} fusion(f32[360,2,1,1440]{3,0,2,1:T(8,128)} %get-tuple-element.6, f32[360,2,1,1440]{3,0,2,1:T(8,128)} %get-tuple-element.5), kind=kLoop, calls=%fused_computation | loop fusion | flops 2073600 | bytes 16588800 | tf_op jit(solution)/shard_map/stack | solution.py:59
  140.3 10.9 %copy.48 = f32[360,2,2,1440]{3,2,1,0:T(2,128)} copy(f32[360,2,2,1440]{3,0,2,1:T(8,128)S(1)} %pad_maximum_fusion) | data formatting | bytes 16588800 | tf_op jit(solution)/shard_map/stack | solution.py:59
  151.2 11.4 %reshape.142 = f32[1440,1440]{1,0:T(8,128)} reshape(f32[360,2,2,1440]{3,2,1,0:T(2,128)} %copy.48) | data formatting | bytes 16588800 | tf_op jit(solution)/shard_map/reshape | solution.py:59
  162.6 8.1 %fusion.17 = f32[105,1440]{1,0:T(8,128)} fusion(f32[1440,105]{1,0:T(8,128)S(1)} %bitcast.24, f32[1440,1440]{1,0:T(8,128)} %reshape.142), kind=kOutput, calls=%fused_computation.28 | convolution fusion | flops 2612736000 | bytes 9504000 | tf_op jit(solution)/shard_map/dot_general | solution.py:90
  (17 shorter events, 2.3 us)
Async XLA Ops:
  1.1 36.9 %copy-start = (s32[360]{0:T(512)S(1)}, s32[360]{0:T(512)}, u32[]{:S(2)}) copy-start(s32[360]{0:T(512)} %param.3) | copy-start | bytes 4324
  2.4 30.0 %all-to-all-start.1 = ((bf16[64,2,1008]{2,1,0:T(2,128)(2,1)}), bf16[64,2,1008]{2,1,0:T(2,128)(2,1)S(1)}, u32[]{:S(2)}, u32[]{:S(2)}) async-start(bf16[64,2,1008]{2,1,0:T(2,128)(2,1)} %reshape.144), calls=%async_computation.1 | async-start | bytes 524288 | tf_op jit(solution)/shard_map/all_to_all | solution.py:77
  32.4 42.2 %all-to-all-start = ((bf16[64,10,768]{2,1,0:T(8,128)(2,1)}), bf16[64,10,768]{2,1,0:T(8,128)(2,1)S(1)}, u32[]{:S(2)}, u32[]{:S(2)}) async-start(bf16[64,10,768]{2,1,0:T(8,128)(2,1)} %concatenate.17), calls=%async_computation | async-start | bytes 3145728 | tf_op jit(solution)/shard_map/all_to_all | solution.py:76
  77.9 41.0 %all-to-all-start.2 = ((f32[1,2,640,168]{3,1,0,2:T(2,128)}), f32[1,2,640,168]{3,1,0,2:T(2,128)S(1)}, u32[]{:S(2)}, u32[]{:S(2)}) async-start(f32[1,2,640,168]{3,1,0,2:T(2,128)} %copy.44), calls=%async_computation.2 | async-start | bytes 2621440 | tf_op jit(solution)/shard_map/all_to_all | solution.py:82
  131.9 30.7 %all-to-all-start.4 = ((f32[4,2,45,2,2,105]{5,4,3,2,1,0:T(2,128)}), f32[4,2,45,2,2,105]{5,4,3,2,1,0:T(2,128)S(1)}, u32[]{:S(2)}, u32[]{:S(2)}) async-start(f32[4,2,45,2,2,105]{5,4,3,2,1,0:T(2,128)} %copy.47), calls=%async_computation.4 | async-start | bytes 1474560 | tf_op jit(solution)/shard_map/all_to_all | solution.py:32
where the time goes:
time: 172 us; the launch traced here: 171 us
  waiting for transfers between devices  53.9 us (31%)
  starting transfers between devices  37.1 us (22%)
  local copies, waits for them, and re-layouts  34.5 us (20%)
  other arithmetic  27 us (16%)
  blocking collectives  9.12 us (5%)
  matrix products  8.94 us (5%)
    all_to_all x1, waiting for transfers between devices, body(): lax.all_to_all(table_pad, 'lat', split_axis=0, concat_axis=1, tiled=True)  34.3 us
    mul x1, other arithmetic, fourier_basis(): real_row = weight * jnp.cos(radians)  21.3 us
    all_to_all x1, starting transfers between devices, body(): lax.all_to_all(coefs_pad, 'lat', split_axis=0, concat_axis=1, tiled=True)  17.1 us
    reshape x1, local copies, waits for them, and re-layouts, fourier_basis(): return jnp.stack([real_row, imag_row], axis=2).reshape(-1, lon_count)  11.4 us
    another operation x1, local copies, waits for them, and re-layouts, fourier_basis(): return jnp.stack([real_row, imag_row], axis=2).reshape(-1, lon_count)  10.9 us
    all_to_all x1, starting transfers between devices, body(): lax.all_to_all(sums, 'lat', split_axis=2, concat_axis=0, tiled=True)  10.3 us
    all_to_all x1, waiting for transfers between devices, body(): lax.all_to_all(coefs_pad, 'lat', split_axis=0, concat_axis=1, tiled=True)  10.2 us
    all_to_all x1, waiting for transfers between devices, body(): lax.all_to_all(sums, 'lat', split_axis=2, concat_axis=0, tiled=True)  9.33 us
  transfers between devices with their start and end apart: 4, of which 3 were waited for; matrix products, arithmetic and copies ran while one was open for 31% of the time, Pallas kernels for 0%

commit v1 on v0

v1 whole, which is shorter than its diff:
```python
import math

import jax
import jax.numpy as jnp
from jax import lax
from jax.experimental import pallas as pl
from jax.experimental.pallas import tpu as pltpu
from jax.sharding import PartitionSpec as P

DEG = 720
LON = 1440
HALF = LON // 2
CH = 84
LAT_DEV = 10
CHUNK = LAT_DEV * CH // 8
MESH = pl.DeviceIdType.MESH
ORDER = (4, 3, 5, 2, 6, 1, 7)
ROWS = 1024
BLK = 64


def wave_rows(pw_ref, tab_ref):
    pw = pw_ref[...]
    half = jnp.broadcast_to((pw >> 1).astype(jnp.float32).astype(jnp.bfloat16), (128, 384))
    low = jnp.broadcast_to((pw & 1).astype(jnp.float32).astype(jnp.bfloat16), (128, 384))

    def step(b, _):
        row = lax.broadcasted_iota(jnp.int32, (256, 384), 0) + b * 256
        col = lax.broadcasted_iota(jnp.int32, (256, 384), 1)
        group = row >> 3
        slot = 3 * (group & 15) + ((row & 7) >> 1)
        slot = (group >> 4) * 45 + jnp.where((slot < 45) & ((row & 7) < 6), slot, 0)
        pick = jnp.where(col == slot, 1.0, 0.0).astype(jnp.bfloat16)
        dims = (((1,), (1,)), ((), ()))
        hi = lax.dot_general(pick, half, dims, preferred_element_type=jnp.float32)
        lo = lax.dot_general(pick, low, dims, preferred_element_type=jnp.float32)
        tab_ref[pl.ds(pl.multiple_of(b * 256, 256), 256), :] = 2.0 * hi + lo
        return 0

    lax.fori_loop(0, ROWS // 256, step, 0)


def cos_sin(phase):
    turns = jnp.floor(phase * (1.0 / LON))
    t = (phase - turns * LON - HALF) * (2.0 * math.pi / LON / 4.0)
    q = t * t
    s = t * (1.0 + q * (-1.0 / 6 + q * (1.0 / 120 + q * (-1.0 / 5040 + q * (1.0 / 362880)))))
    c = 1.0 + q * (-0.5 + q * (1.0 / 24 + q * (-1.0 / 720 + q * (1.0 / 40320 - q * (1.0 / 3628800)))))
    s, c = 2.0 * s * c, 1.0 - 2.0 * s * s
    s, c = 2.0 * s * c, 1.0 - 2.0 * s * s
    return -c, -s


def basis_block(b, tab_ref, hi_ref, lo_ref):
    start = pl.multiple_of(b * BLK, BLK)
    u = tab_ref[pl.ds(start, BLK), :]
    lane = lax.broadcasted_iota(jnp.int32, (BLK, 128), 1).astype(jnp.float32)
    part = (lax.broadcasted_iota(jnp.int32, (BLK, 128), 0) & 1).astype(jnp.float32)
    odd = u - 2.0 * jnp.floor(u * 0.5)
    for h in range(2):
        wave = jnp.where(odd == float(h), u, float(DEG - 1) - u)
        c, s = cos_sin(wave * lane + 360.0 * part)
        weight = jnp.where(wave == 0.0, 1.0, 2.0)
        c, s = c * weight, s * weight
        cj, sj = cos_sin(wave * 128.0)
        for j in range(6):
            high = c.astype(jnp.bfloat16)
            hi_ref[h, pl.ds(start, BLK), 128 * j : 128 * j + 128] = high
            lo_ref[h, pl.ds(start, BLK), 128 * j : 128 * j + 128] = (c - high.astype(jnp.float32)).astype(jnp.bfloat16)
            if j < 5:
                c, s = c * cj - s * sj, s * cj + c * sj


def legendre_sums(waves, table_ref, coef_ref, sums_ref, out_ref):
    table = table_ref[...].reshape(256, 768)
    row = lax.broadcasted_iota(jnp.int32, (768, 168), 0)
    for s in range(3):
        coefs = coef_ref[..., 168 * s : 168 * s + 168].reshape(768, 168)
        u = waves[s]
        odd = lax.rem(u, 2)
        first = DEG - u
        for h in range(2):
            low = jnp.where(odd == h, 0, first)
            high = jnp.where(odd == h, first, DEG + 1)
            kept = jnp.where((row >= low) & (row < high), coefs, jnp.zeros((), coefs.dtype))
            sums = jnp.dot(table, kept, preferred_element_type=jnp.float32)
            for e in range(2):
                sums_ref[6 * h + 2 * s + e, :, 0:CH] = sums[:, CH * e : CH * e + CH]
    lane = lax.broadcasted_iota(jnp.int32, (8, 128), 1)
    for h in range(2):
        for s in range(3):
            for e in range(2):
                lats = [
                    sums_ref[6 * h + 2 * s + e, pl.ds(LAT_DEV * s + i, 8, stride=32), :] for i in range(LAT_DEV)
                ]
                for k in range(8):
                    i, off = divmod(CHUNK * k, CH)
                    a = lats[i] if off == 0 else pltpu.roll(lats[i], 128 - off, 1)
                    b = pltpu.roll(lats[i + 1], CH - off, 1)
                    chunk = jnp.where(lane < CH - off, a, b)
                    out_ref[pl.ds(16 * k + 8 * h + 2 * s + e, 8, stride=128), :] = chunk


def kernel(pw_s, pw_v, table_in, coef_in, out_ref, tab, hi, lo, table_a, table_b, coef_a, coef_b, sums_s, send, home, held,
           cs, cr, ts, tr, rs, rr, fs, fr, ms, mr):
    lat = lax.axis_index("lat")
    ma = lax.axis_index("ma")
    y, z = lat // 8, lax.rem(lat, 8)
    along_z = [(y * 8 + lax.rem(z + d, 8), ma) for d in range(8)]
    along_y = [(lax.rem(y + d, 8) * 8 + z, ma) for d in range(8)]
    along_ma = [(lat, lax.rem(ma + d, 8)) for d in range(8)]

    barrier = pltpu.get_barrier_semaphore()
    for peers in (along_z, along_y, along_ma):
        for d in range(1, 8):
            pl.semaphore_signal(barrier, inc=1, device_id=peers[d], device_id_type=MESH)
    wave_rows(pw_v, tab)
    send[...] = jnp.zeros_like(send)
    pl.semaphore_wait(barrier, 21)

    def copy(src, dst, s_sem, r_sem, to):
        return pltpu.make_async_remote_copy(
            src_ref=src, dst_ref=dst, send_sem=s_sem, recv_sem=r_sem, device_id=to, device_id_type=MESH
        )

    waits = []
    first = []
    for d in ORDER:
        za, yb = lax.rem(z + d, 8), lax.rem(y + d, 8)
        a = copy(coef_in.at[za], coef_a.at[y, z], cs.at[0, d], cr.at[0, d], along_z[d])
        b = copy(coef_in.at[8 + yb], coef_b.at[y, z], cs.at[1, d], cr.at[1, d], along_y[d])
        a.start()
        b.start()
        first += [a, b]
    coef_a[y, z] = coef_in[z]
    coef_b[y, z] = coef_in[8 + y]

    tables = []

    def send_tables(ds):
        for d in ds:
            za, yb = lax.rem(z + d, 8), lax.rem(y + d, 8)
            a = copy(table_in.at[za], table_a.at[z], ts.at[0, d], tr.at[0, d], along_z[d])
            b = copy(table_in.at[8 + yb], table_b.at[y], ts.at[1, d], tr.at[1, d], along_y[d])
            a.start()
            b.start()
            tables.extend([a, b])

    def basis(lo_b, hi_b):
        def step(b, _):
            basis_block(b, tab, hi, lo)
            return 0

        lax.fori_loop(lo_b, hi_b, step, 0)

    send_tables(ORDER[:2])
    basis(0, 3)
    for c in first:
        c.wait_recv()
    waits += first

    for s in range(4):
        now = []
        for way in range(2):
            if way == 1 and s == 3:
                continue
            sign = 1 if way == 0 else 7
            by, bz = lax.rem(y + (8 - sign) * s, 8), lax.rem(z + (8 - sign) * s, 8)
            a = copy(coef_a.at[by], coef_a.at[by], rs.at[0, way, s], rr.at[0, way, s], along_y[sign])
            b = copy(coef_b.at[:, bz], coef_b.at[:, bz], rs.at[1, way, s], rr.at[1, way, s], along_z[sign])
            a.start()
            b.start()
            now += [a, b]
        send_tables(ORDER[2 + 2 * s : 4 + 2 * s] if s < 2 else ORDER[6:7] if s == 2 else ())
        basis(3 + 3 * s, 6 + 3 * s if s < 3 else ROWS // BLK)
        for c in now:
            c.wait_recv()
        waits += now
    table_a[z] = table_in[z]
    table_b[y] = table_in[8 + y]

    sums = []
    for half, (table, coef, mine, peers) in enumerate(
        ((table_a, coef_a, z, along_z), (table_b, coef_b, y, along_y))
    ):
        for c in tables[half::2]:
            c.wait_recv()
        at = ma * 45 + half * 24 + mine * 3
        waves = [pw_s[jnp.minimum(at + s, 359)] for s in range(3)]
        legendre_sums(waves, table, coef, sums_s, send.at[half])
        for d in ORDER:
            to = lax.rem(mine + d, 8)
            c = copy(
                send.at[half, pl.ds(pl.multiple_of(to * 128, 128), 128)],
                home.at[half * 8 + mine],
                fs.at[half, d],
                fr.at[half, d],
                peers[d],
            )
            c.start()
            sums.append(c)
        home[half * 8 + mine] = send[half, pl.ds(pl.multiple_of(mine * 128, 128), 128)]
    waits += tables
    for c in sums:
        c.wait_recv()
    waits += sums

    final = []
    for d in ORDER:
        to = lax.rem(ma + d, 8)
        c = copy(
            home.at[:, pl.ds(pl.multiple_of(to * 16, 16), 16)], held.at[ma], ms.at[d], mr.at[d], along_ma[d]
        )
        c.start()
        final.append(c)
    held[ma] = home[:, pl.ds(pl.multiple_of(ma * 16, 16), 16), :]
    for c in final:
        c.wait_recv()
    waits += final
    for c in waits:
        c.wait_send()

    dims = (((0,), (0,)), ((), ()))
    halves = []
    for h in range(2):
        x = held[:, :, 8 * h : 8 * h + 8, :].reshape(ROWS, 128)
        high = x.astype(jnp.bfloat16)
        low = (x - high.astype(jnp.float32)).astype(jnp.bfloat16)
        total = lax.dot_general(high, hi[h], dims, preferred_element_type=jnp.float32)
        total += lax.dot_general(low, hi[h], dims, preferred_element_type=jnp.float32)
        total += lax.dot_general(high, lo[h], dims, preferred_element_type=jnp.float32)
        halves.append(total)
    out_ref[:, 0:HALF] = (halves[0] + halves[1])[:CHUNK, :HALF]
    out_ref[:, HALF:LON] = (halves[0] - halves[1])[:CHUNK, :HALF]


def body(pair_wave, legendre, coefs):
    table = jnp.pad(legendre, ((0, 3), (0, 0), (0, 0))).reshape(16, 30, 768)
    table = jnp.pad(table, ((0, 0), (0, 2), (0, 0)))
    coef = jnp.pad(coefs, ((0, 3), (0, 0), (0, 0))).reshape(16, 3, 12, 168)
    coef = jnp.transpose(coef, (0, 2, 1, 3)).reshape(16, 12, 504)
    coef = jnp.pad(coef, ((0, 0), (0, 0), (0, 8))).reshape(16, 3, 4, 512)
    pw_v = jnp.pad(pair_wave, (0, 24)).reshape(1, 384)
    vmem = pl.BlockSpec(memory_space=pltpu.VMEM)
    bf16, f32, dma = jnp.bfloat16, jnp.float32, pltpu.SemaphoreType.DMA
    return pl.pallas_call(
        kernel,
        out_shape=jax.ShapeDtypeStruct((CHUNK, LON), f32),
        in_specs=[pl.BlockSpec(memory_space=pltpu.SMEM), vmem, vmem, vmem],
        out_specs=vmem,
        scratch_shapes=[
            pltpu.VMEM((ROWS, 128), f32),
            pltpu.VMEM((2, ROWS, 768), bf16),
            pltpu.VMEM((2, ROWS, 768), bf16),
            pltpu.VMEM((8, 32, 768), bf16),
            pltpu.VMEM((8, 32, 768), bf16),
            pltpu.VMEM((8, 8, 3, 4, 512), bf16),
            pltpu.VMEM((8, 8, 3, 4, 512), bf16),
            pltpu.VMEM((12, 256, 128), f32),
            pltpu.VMEM((2, 1024, 128), f32),
            pltpu.VMEM((16, 128, 128), f32),
            pltpu.VMEM((8, 16, 16, 128), f32),
            dma((2, 8)), dma((2, 8)), dma((2, 8)), dma((2, 8)),
            dma((2, 2, 4)), dma((2, 2, 4)), dma((2, 8)), dma((2, 8)), dma((8,)), dma((8,)),
        ],
        compiler_params=pltpu.CompilerParams(
            collective_id=0, has_side_effects=True, vmem_limit_bytes=60 * 2**20
        ),
    )(pair_wave, pw_v, table, coef)


def solution(mesh):
    placed = (P(), P("ma", "lat", None), P("ma", "lat", None))
    return jax.shard_map(
        body, mesh=mesh, in_specs=placed, out_specs=P(("lat", "ma"), None), check_vma=False
    )
```

time: 172 us -> 81.1 us (0.47)
  Pallas kernels: 0 us -> 74.3 us
  waiting for transfers between devices: 53.9 us -> 0 us
  starting transfers between devices: 37.1 us -> 0 us
  local copies, waits for them, and re-layouts: 34.5 us -> 6.51 us
  other arithmetic: 27 us -> 0 us
  blocking collectives: 9.12 us -> 0 us
  matrix products: 8.94 us -> 0 us
    pallas_call x0 -> x1, Pallas kernels: none -> 74.3 us  [body(): pl.pallas_call(kernel, out_shape=jax.ShapeDtypeStruct((CHUNK, LON), f32),...]
    all_to_all x4 -> x0, waiting for transfers between devices: 53.9 us -> none  [the longest x1 34.3 us: body(): lax.all_to_all(table_pad, 'lat', split_axis=0, concat_axis=1, tiled=True)]
    all_to_all x4 -> x0, starting transfers between devices: 37.1 us -> none  [the longest x1 17.1 us: body(): lax.all_to_all(coefs_pad, 'lat', split_axis=0, concat_axis=1, tiled=True)]
    mul x1 -> x0, other arithmetic: 21.3 us -> none  [fourier_basis(): real_row = weight * jnp.cos(radians)]
    another operation x5 -> x0, local copies, waits for them, and re-layouts: 11.7 us -> none  [the longest x1 10.9 us: fourier_basis(): return jnp.stack([real_row, imag_row], axis=2).reshape(-1, lon_count)]
    reshape x4 -> x5, local copies, waits for them, and re-layouts: 13.1 us -> 2.01 us  [the longest x1 0.83 us: body(): coef = jnp.pad(coef, ((0, 0), (0, 0), (0, 8))).reshape(16, 3, 4, 512)]
    all_to_all x1 -> x0, blocking collectives: 9.12 us -> none  [moved_by_axis(): lax.all_to_all(pieces, axes[k], split_axis=k, concat_axis=k, tiled=True)]
    dot_general x2 -> x0, matrix products: 8.94 us -> none  [the longest x1 8.11 us: body(): lax.dot_general(fourier_rows, synth_basis, (((0,), (0,)), ((), ())), prec...]
  transfers between devices with their start and end apart: 4 -> 0, of which waited for: 3 -> 0; matrix products, arithmetic and copies ran while one was open for 31% -> 0% of each run, Pallas kernels for 0% -> 0%
where the time goes in v1:
time: 81.1 us; the launch traced here: 80.9 us
  Pallas kernels  74.3 us (92%)
  local copies, waits for them, and re-layouts  6.51 us (8%)
    pallas_call x1, Pallas kernels, body(): pl.pallas_call(kernel, out_shape=jax.ShapeDtypeStruct((CHUNK, LON), f32),...  74.3 us
    unnamed x6, local copies, waits for them, and re-layouts  3.36 us

profile of v1, /device:TPU:1, one launch (start us, length us, event | category | flops | bytes accessed | tf_op | source)
XLA Modules:
  0.0 80.9 jit_solution(17120272270873386625)
XLA Ops:
  0.0 1.4 %copy.8 = bf16[45,10,768]{2,1,0:T(8,128)(2,1)S(1)} copy(bf16[45,10,768]{2,0,1:T(8,128)(2,1)} %param.4) | data formatting | bytes 1382400
  1.4 0.1 pad.21.clone
  1.5 0.2 reshape.16
  1.7 0.0 copy-start
  1.7 1.0 %pad.22.table_in = bf16[16,32,768]{2,1,0:T(8,128)(2,1)} pad(bf16[16,30,768]{2,1,0:T(8,128)(2,1)S(1)} %reshape.16, bf16[]{:T(256)} %constant.3.clone.1), padding=0_0x0_2x0_0 | pad | bytes 1523714 | tf_op jit(solution)/shard_map/jit(_pad)/pad | solution.py:239
  2.7 0.0 copy-done
  2.7 0.1 pad.23
  2.7 0.0 copy-start.1
  2.7 0.2 reshape.17
  2.9 0.2 reshape.18
  3.2 0.8 %copy.7.coef_in = bf16[16,3,4,512]{3,2,1,0:T(4,128)(2,1)} copy(bf16[16,3,4,512]{3,0,2,1:T(8,128)(2,1)S(1)} %bitcast.7) | data formatting | bytes 393216 | tf_op jit(solution)/shard_map/reshape | solution.py:242
  4.0 0.0 copy-done.1
  4.0 0.6 reshape.15.pw_v
  4.6 74.3 %shard_map.37 = f32[105,1440]{1,0:T(8,128)} custom-call(s32[360]{0:T(512)} %pw_s.1, s32[1,384]{1,0:T(1,128)} %reshape.15.pw_v, bf16[16,32,768]{2,1,0:T(8,128)(2,1)} %pad.22.table_in, bf16[16,3,4,512]{3,2,1,0:T(4,128)(2,1)} %copy.7.coef_in), custom_call_target="tpu_custom_call" | custom-call | tf_op jit(solution)/shard_map/pallas_call | solution.py:246
  78.9 2.0 %copy.10 = f32[105,1440]{1,0:T(8,128)} copy(f32[105,1440]{1,0:T(8,128)} %shard_map.37) | data formatting | bytes 1209600
  (2 shorter events, 0.0 us)
Async XLA Ops:
  1.7 1.0 %copy-start = (bf16[45,12,168]{2,0,1:T(8,128)(2,1)S(1)}, bf16[45,12,168]{2,0,1:T(8,128)(2,1)}, u32[]{:S(2)}) copy-start(bf16[45,12,168]{2,0,1:T(8,128)(2,1)} %param.5) | copy-start | bytes 544324
  2.7 1.3 %copy-start.1 = (s32[360]{0:T(512)S(1)}, s32[360]{0:T(512)}, u32[]{:S(2)}) copy-start(s32[360]{0:T(512)} %pw_s.1) | copy-start | bytes 4324

commit v2 on v1

v2 whole, which is shorter than its diff:
```python
import math

import jax
import jax.numpy as jnp
from jax import lax
from jax.experimental import pallas as pl
from jax.experimental.pallas import tpu as pltpu
from jax.sharding import PartitionSpec as P

DEG = 720
LON = 1440
HALF = LON // 2
CH = 84
LAT_DEV = 10
CHUNK = LAT_DEV * CH // 8
MESH = pl.DeviceIdType.MESH
ORDER = (4, 3, 5, 2, 6, 1, 7)
ROWS = 1024
BLK = 64


def wave_rows(pw_s, pw_v, tab_ref):
    lane = lax.broadcasted_iota(jnp.int32, (8, 128), 1)
    for t in range(3):

        def gather(n, v):
            for k in range(8):
                at = t * 128 + n * 8 + k
                v = jnp.where(lane == n * 8 + k, pw_s[jnp.minimum(at, 359)], v)
            return v

        pw_v[:, 128 * t : 128 * t + 128] = lax.fori_loop(0, 16, gather, jnp.zeros((8, 128), jnp.int32))
    pw = pw_v[0:1, :]
    half = jnp.broadcast_to((pw >> 1).astype(jnp.float32).astype(jnp.bfloat16), (128, 384))
    low = jnp.broadcast_to((pw & 1).astype(jnp.float32).astype(jnp.bfloat16), (128, 384))

    def step(b, _):
        row = lax.broadcasted_iota(jnp.int32, (256, 384), 0) + b * 256
        col = lax.broadcasted_iota(jnp.int32, (256, 384), 1)
        group = row >> 3
        slot = 24 * (group >> 6) + 3 * (group & 7) + ((row & 7) >> 1)
        slot = ((group >> 3) & 7) * 45 + jnp.where((slot < 45) & ((row & 7) < 6), slot, 0)
        pick = jnp.where(col == slot, 1.0, 0.0).astype(jnp.bfloat16)
        dims = (((1,), (1,)), ((), ()))
        hi = lax.dot_general(pick, half, dims, preferred_element_type=jnp.float32)
        lo = lax.dot_general(pick, low, dims, preferred_element_type=jnp.float32)
        tab_ref[pl.ds(pl.multiple_of(b * 256, 256), 256), :] = 2.0 * hi + lo
        return 0

    lax.fori_loop(0, ROWS // 256, step, 0)


def cos_sin(phase):
    turns = jnp.floor(phase * (1.0 / LON))
    t = (phase - turns * LON - HALF) * (2.0 * math.pi / LON / 4.0)
    q = t * t
    s = t * (1.0 + q * (-1.0 / 6 + q * (1.0 / 120 + q * (-1.0 / 5040 + q * (1.0 / 362880)))))
    c = 1.0 + q * (-0.5 + q * (1.0 / 24 + q * (-1.0 / 720 + q * (1.0 / 40320 - q * (1.0 / 3628800)))))
    s, c = 2.0 * s * c, 1.0 - 2.0 * s * s
    s, c = 2.0 * s * c, 1.0 - 2.0 * s * s
    return -c, -s


def basis_block(b, tab_ref, hi_ref, lo_ref):
    start = pl.multiple_of(b * BLK, BLK)
    u = tab_ref[pl.ds(start, BLK), :]
    lane = lax.broadcasted_iota(jnp.int32, (BLK, 128), 1).astype(jnp.float32)
    part = (lax.broadcasted_iota(jnp.int32, (BLK, 128), 0) & 1).astype(jnp.float32)
    odd = u - 2.0 * jnp.floor(u * 0.5)
    for h in range(2):
        wave = jnp.where(odd == float(h), u, float(DEG - 1) - u)
        c, s = cos_sin(wave * lane + 360.0 * part)
        weight = jnp.where(wave == 0.0, 1.0, 2.0)
        c, s = c * weight, s * weight
        cj, sj = cos_sin(wave * 128.0)
        for j in range(6):
            high = c.astype(jnp.bfloat16)
            hi_ref[h, pl.ds(start, BLK), 128 * j : 128 * j + 128] = high
            lo_ref[h, pl.ds(start, BLK), 128 * j : 128 * j + 128] = (c - high.astype(jnp.float32)).astype(jnp.bfloat16)
            if j < 5:
                c, s = c * cj - s * sj, s * cj + c * sj


def pack_tables(raw, wide, rows, out):
    for t in range(6):
        cols = slice(128 * t, 128 * t + 128)
        for i in range(LAT_DEV):
            wide[t, 48 * i : 48 * i + 45, :] = raw[i, :, cols].astype(jnp.float32)
            wide[t, 48 * i + 45 : 48 * i + 48, :] = jnp.zeros((3, 128), jnp.float32)
        for half in range(2):
            for s in range(3):
                for i in range(LAT_DEV):
                    got = wide[t, pl.ds(48 * i + 24 * half + s, 8, stride=3), :]
                    rows[t, pl.ds(256 * half + 3 * i + s, 8, stride=32), :] = got
            for k in (30, 31):
                rows[t, pl.ds(256 * half + k, 8, stride=32), :] = jnp.zeros((8, 128), jnp.float32)
        out[:, :, cols] = rows[t].astype(jnp.bfloat16).reshape(16, 32, 128)


def pack_coefs(raw, wide, rows, out):
    for j in range(12):
        for t, (at, size) in enumerate(((0, 128), (128, 40))):
            wide[t, 48 * j : 48 * j + 45, 0:size] = raw[j, :, at : at + size].astype(jnp.float32)
            wide[t, 48 * j + 45 : 48 * j + 48, 0:size] = jnp.zeros((3, size), jnp.float32)
    for half in range(2):
        for j in range(12):
            parts = []
            for s in range(3):
                parts.append(wide[0, pl.ds(48 * j + 24 * half + s, 8, stride=3), :])
                parts.append(wide[1, pl.ds(48 * j + 24 * half + s, 8, stride=3), :][:, 0:40])
            parts.append(jnp.zeros((8, 8), jnp.float32))
            line = jnp.concatenate(parts, axis=1)
            for t in range(4):
                rows[t, pl.ds(96 * half + j, 8, stride=12), :] = line[:, 128 * t : 128 * t + 128]
    for t in range(4):
        out[:, :, :, 128 * t : 128 * t + 128] = rows[t].astype(jnp.bfloat16).reshape(16, 3, 4, 128)


def legendre_sums(waves, table_ref, coef_ref, sums_ref, rows_ref, out_ref):
    table = table_ref[...].reshape(256, 768)
    row = lax.broadcasted_iota(jnp.int32, (768, 168), 0)
    col = lax.broadcasted_iota(jnp.int32, (768, 168), 1)
    for s in range(3):
        coefs = coef_ref[..., 168 * s : 168 * s + 168].reshape(768, 168)
        u = waves[s]
        odd = lax.rem(u, 2)
        first = DEG - u
        for h in range(2):
            low = jnp.where(odd == h, 0, first)
            high = jnp.where(odd == h, first, DEG + 1)
            kept = jnp.where((row >= low) & (row < high), coefs, jnp.zeros((), coefs.dtype))
            sums = jnp.dot(table, kept, preferred_element_type=jnp.float32)
            for e in range(2):
                sums_ref[6 * h + 2 * s + e, :, 0:CH] = sums[:, CH * e : CH * e + CH]
    lane = lax.broadcasted_iota(jnp.int32, (8, 128), 1)
    for h in range(2):
        for s in range(3):
            for e in range(2):
                lats = [sums_ref[6 * h + 2 * s + e, pl.ds(3 * i + s, 8, stride=32), :] for i in range(LAT_DEV)]
                for k in range(8):
                    i, off = divmod(CHUNK * k, CH)
                    a = lats[i] if off == 0 else pltpu.roll(lats[i], 128 - off, 1)
                    b = pltpu.roll(lats[i + 1], CH - off, 1)
                    chunk = jnp.where(lane < CH - off, a, jnp.where(lane < CHUNK, b, 0.0))
                    rows_ref[pl.ds(16 * k + 8 * h + 2 * s + e, 8, stride=128), :] = chunk
    lanes = lax.broadcasted_iota(jnp.int32, (128, 128), 1)
    for b in range(8):
        x = rows_ref[128 * b : 128 * b + 128, :]
        top = jnp.maximum(jnp.max(jnp.abs(x), axis=1, keepdims=True), 1e-37)
        level = jnp.ceil(8.0 * jnp.log2(top) + 0.01)
        x = jnp.floor(x * jnp.exp2(level * -0.125) * 32767.0 + 0.5)
        x = jnp.where(lanes == CHUNK, level, x)
        out_ref[8 * b : 8 * b + 8] = x.astype(jnp.int32).astype(jnp.int16).reshape(8, 16, 128)


def kernel(pw_s, table_hbm, coef_hbm, out_ref, table_raw, coef_raw, wide_t, rows_t, wide_c, rows_c, table_in, coef_in,
           pw_v, tab, hi, lo, table_a, table_b, coef_a, coef_b, sums_s, rows_s, send, held,
           lsem, cs, cr, ts, tr, rs, rr, fs, fr):
    lat = lax.axis_index("lat")
    ma = lax.axis_index("ma")
    y, z = lat // 8, lax.rem(lat, 8)
    along_z = [(y * 8 + lax.rem(z + d, 8), ma) for d in range(8)]
    along_y = [(lax.rem(y + d, 8) * 8 + z, ma) for d in range(8)]
    along_ma = [(lat, lax.rem(ma + d, 8)) for d in range(8)]

    get_coefs = pltpu.make_async_copy(coef_hbm, coef_raw, lsem.at[0])
    get_coefs.start()
    get_table = pltpu.make_async_copy(table_hbm, table_raw, lsem.at[1])
    get_table.start()
    barrier = pltpu.get_barrier_semaphore()
    for peers in (along_z, along_y, along_ma):
        for d in range(1, 8):
            pl.semaphore_signal(barrier, inc=1, device_id=peers[d], device_id_type=MESH)
    get_coefs.wait()
    pack_coefs(coef_raw, wide_c, rows_c, coef_in)
    pl.semaphore_wait(barrier, 21)

    def copy(src, dst, s_sem, r_sem, to):
        return pltpu.make_async_remote_copy(
            src_ref=src, dst_ref=dst, send_sem=s_sem, recv_sem=r_sem, device_id=to, device_id_type=MESH
        )

    sent = []

    def launch(c):
        c.start()
        sent.append(c)
        return c

    for d in ORDER:
        za, yb = lax.rem(z + d, 8), lax.rem(y + d, 8)
        launch(copy(coef_in.at[za], coef_a.at[y, z], cs.at[0, d], cr.at[0, d], along_z[d]))
        launch(copy(coef_in.at[8 + yb], coef_b.at[y, z], cs.at[1, d], cr.at[1, d], along_y[d]))
    coef_a[y, z] = coef_in[z]
    coef_b[y, z] = coef_in[8 + y]
    get_table.wait()
    pack_tables(table_raw, wide_t, rows_t, table_in)

    tables = []

    def send_tables(ds):
        for d in ds:
            za, yb = lax.rem(z + d, 8), lax.rem(y + d, 8)
            tables.append(launch(copy(table_in.at[za], table_a.at[z], ts.at[0, d], tr.at[0, d], along_z[d])))
            tables.append(launch(copy(table_in.at[8 + yb], table_b.at[y], ts.at[1, d], tr.at[1, d], along_y[d])))

    def basis(b):
        basis_block(b, tab, hi, lo)

    send_tables(ORDER[:2])
    wave_rows(pw_s, pw_v, tab)
    rows_s[...] = jnp.zeros_like(rows_s)

    def chunk_here(half, mine, at, peers):
        d = lax.rem(mine - at + 8, 8)
        copy(coef_in.at[0], coef_a.at[0, 0], cs.at[half, d], cr.at[half, d], peers[1]).wait_recv()

    arriving = {}
    for s in range(4):
        for k, turn in enumerate((0, 1, 3, 2)):
            pz, py = lax.rem(z // 2 + turn, 4), lax.rem(y // 2 + turn, 4)
            if s == 0:
                if turn == 0:
                    chunk_here(0, z, z + 1 - 2 * lax.rem(z, 2), along_z)
                    chunk_here(1, y, y + 1 - 2 * lax.rem(y, 2), along_y)
                else:
                    for n in range(2):
                        chunk_here(0, z, 2 * pz + n, along_z)
                        chunk_here(1, y, 2 * py + n, along_y)
            for way in range(2):
                if s == 3 and (k < 2) != (way == 0):
                    continue
                if s > 0:
                    for c in arriving.pop((s - 1, k, way)):
                        c.wait_recv()
                sign = 1 if way == 0 else 7
                by, bz = lax.rem(y + (8 - sign) * s, 8), lax.rem(z + (8 - sign) * s, 8)
                arriving[s, k, way] = []
                ref_a = coef_a.at[by, pl.ds(2 * pz, 2)]
                ref_b = coef_b.at[pl.ds(2 * py, 2), bz]
                a = copy(ref_a, ref_a, rs.at[0, way, s, k], rr.at[0, way, s, k], along_y[sign])
                b = copy(ref_b, ref_b, rs.at[1, way, s, k], rr.at[1, way, s, k], along_z[sign])
                arriving[s, k, way] += [launch(a), launch(b)]
            basis(4 * s + k)
        send_tables(ORDER[2 + 2 * s : 4 + 2 * s])
    for cs_ in arriving.values():
        for c in cs_:
            c.wait_recv()
    table_a[z] = table_in[z]
    table_b[y] = table_in[8 + y]

    sets = ((table_a, coef_a, z, along_z), (table_b, coef_b, y, along_y))
    for half, (table, coef, mine, peers) in enumerate(sets):
        for c in tables[half::2]:
            c.wait_recv()
        at = ma * 45 + half * 24 + mine * 3
        waves = [pw_s[jnp.minimum(at + s, 359)] for s in range(3)]
        legendre_sums(waves, table, coef, sums_s, rows_s, send.at[half])
        for d in ORDER + (0,):
            to = lax.rem(mine + d, 8)

            def step(n, _, d=d, to=to, half=half, mine=mine, peers=peers):
                m2 = lax.rem(ma + n, 8)
                copy(
                    send.at[half, to * 8 + m2], held.at[half, ma * 8 + mine], fs.at[half], fr.at[half], (peers[d][0], m2)
                ).start()
                return 0

            lax.fori_loop(0 if d else 1, 8, step, 0)
        held[half, ma * 8 + mine] = send[half, mine * 8 + ma]

    dims = (((0,), (0,)), ((), ()))
    totals = [None, None]
    for half in range(2):
        most = pl.ds(0, 63)
        copy(send.at[half, most], held.at[half, most], fs.at[half], fr.at[half], along_z[1]).wait_recv()
        for h in range(2):
            x = held[half].astype(jnp.int32).astype(jnp.float32)[:, 8 * h : 8 * h + 8, :].reshape(512, 128)
            x = x * (jnp.exp2(x[:, CHUNK : CHUNK + 1] * 0.125) * (1.0 / 32767.0))
            high = x.astype(jnp.bfloat16)
            low = (x - high.astype(jnp.float32)).astype(jnp.bfloat16)
            b_hi, b_lo = hi[h, 512 * half : 512 * half + 512, :], lo[h, 512 * half : 512 * half + 512, :]
            total = lax.dot_general(high, b_hi, dims, preferred_element_type=jnp.float32)
            total += lax.dot_general(low, b_hi, dims, preferred_element_type=jnp.float32)
            total += lax.dot_general(high, b_lo, dims, preferred_element_type=jnp.float32)
            totals[h] = total if half == 0 else totals[h] + total
    out_ref[:, 0:HALF] = (totals[0] + totals[1])[:CHUNK, :HALF]
    out_ref[:, HALF:LON] = (totals[0] - totals[1])[:CHUNK, :HALF]
    for c in sent:
        c.wait_send()
    for half in range(2):
        copy(send.at[half, most], held.at[half, most], fs.at[half], fr.at[half], along_z[1]).wait_send()


def body(pair_wave, legendre, coefs):
    vmem, hbm = pl.BlockSpec(memory_space=pltpu.VMEM), pl.BlockSpec(memory_space=pl.ANY)
    bf16, f32, dma = jnp.bfloat16, jnp.float32, pltpu.SemaphoreType.DMA
    return pl.pallas_call(
        kernel,
        out_shape=jax.ShapeDtypeStruct((CHUNK, LON), f32),
        in_specs=[pl.BlockSpec(memory_space=pltpu.SMEM), hbm, hbm],
        out_specs=vmem,
        scratch_shapes=[
            pltpu.VMEM((LAT_DEV, 45, 768), bf16),
            pltpu.VMEM((12, 45, 168), bf16),
            pltpu.VMEM((6, 480, 128), f32),
            pltpu.VMEM((6, 512, 128), f32),
            pltpu.VMEM((2, 576, 128), f32),
            pltpu.VMEM((4, 192, 128), f32),
            pltpu.VMEM((16, 32, 768), bf16),
            pltpu.VMEM((16, 3, 4, 512), bf16),
            pltpu.VMEM((8, 384), jnp.int32),
            pltpu.VMEM((ROWS, 128), f32),
            pltpu.VMEM((2, ROWS, 768), bf16),
            pltpu.VMEM((2, ROWS, 768), bf16),
            pltpu.VMEM((8, 32, 768), bf16),
            pltpu.VMEM((8, 32, 768), bf16),
            pltpu.VMEM((8, 8, 3, 4, 512), bf16),
            pltpu.VMEM((8, 8, 3, 4, 512), bf16),
            pltpu.VMEM((12, 256, 128), f32),
            pltpu.VMEM((1024, 128), f32),
            pltpu.VMEM((2, 64, 16, 128), jnp.int16),
            pltpu.VMEM((2, 64, 16, 128), jnp.int16),
            dma((2,)),
            dma((2, 8)), dma((2, 8)), dma((2, 8)), dma((2, 8)),
            dma((2, 2, 4, 4)), dma((2, 2, 4, 4)), dma((2,)), dma((2,)),
        ],
        compiler_params=pltpu.CompilerParams(
            collective_id=0, has_side_effects=True, vmem_limit_bytes=60 * 2**20
        ),
    )(pair_wave, jnp.transpose(legendre, (1, 0, 2)), jnp.transpose(coefs, (1, 0, 2)))


def solution(mesh):
    placed = (P(), P("ma", "lat", None), P("ma", "lat", None))
    return jax.shard_map(
        body, mesh=mesh, in_specs=placed, out_specs=P(("lat", "ma"), None), check_vma=False
    )
```

time: 81.1 us -> 60.1 us (0.74)
  Pallas kernels: 74.3 us -> 57.9 us
  local copies, waits for them, and re-layouts: 6.51 us -> 2 us
    pallas_call x1, Pallas kernels: 74.3 us -> 57.9 us  [body(): pl.pallas_call(kernel, out_shape=jax.ShapeDtypeStruct((CHUNK, LON), f32),...]
    reshape x5 -> x0, local copies, waits for them, and re-layouts: 2.01 us -> none  [the longest x1 0.83 us: body(): coef = jnp.pad(coef, ((0, 0), (0, 0), (0, 8))).reshape(16, 3, 4, 512)]
    unnamed x6 -> x1, local copies, waits for them, and re-layouts: 3.36 us -> 2 us
    pad x5 -> x0, local copies, waits for them, and re-layouts: 1.13 us -> none  [the longest x1 0.95 us: body(): table = jnp.pad(table, ((0, 0), (0, 2), (0, 0)))]
where the time goes in v2:
time: 60.1 us; the launch traced here: 59.9 us
  Pallas kernels  57.9 us (96%)
  local copies, waits for them, and re-layouts  2 us (3%)
    pallas_call x1, Pallas kernels, body(): pl.pallas_call(kernel, out_shape=jax.ShapeDtypeStruct((CHUNK, LON), f32),...  57.9 us
    unnamed x1, local copies, waits for them, and re-layouts  2 us

profile of v2, /device:TPU:1, one launch (start us, length us, event | category | flops | bytes accessed | tf_op | source)
XLA Modules:
  0.0 59.9 jit_solution(3810379111656508547)
XLA Ops:
  0.0 57.9 %shard_map.37 = f32[105,1440]{1,0:T(8,128)} custom-call(s32[360]{0:T(512)} %pw_s.1, bf16[10,45,768]{2,1,0:T(8,128)(2,1)} %bitcast.2, bf16[12,45,168]{2,1,0:T(8,128)(2,1)} %bitcast.3), custom_call_target="tpu_custom_call" | custom-call | tf_op jit(solution)/shard_map/pallas_call | solution.py:298
  57.9 2.0 %copy.5 = f32[105,1440]{1,0:T(8,128)} copy(f32[105,1440]{1,0:T(8,128)} %shard_map.37) | data formatting | bytes 1209600

commit v3 on v2

--- a/solution.py
+++ b/solution.py
@@ -16,6 +16,7 @@
 MESH = pl.DeviceIdType.MESH
 ORDER = (4, 3, 5, 2, 6, 1, 7)
 ROWS = 1024
+SENDS = (((4, 3), (5, 2), (6, 1), (7,), ()), ((4, 3), (5, 2), (6, 1), (7,), ()))
 BLK = 64
 
 
@@ -37,9 +38,9 @@
     def step(b, _):
         row = lax.broadcasted_iota(jnp.int32, (256, 384), 0) + b * 256
         col = lax.broadcasted_iota(jnp.int32, (256, 384), 1)
-        group = row >> 3
-        slot = 24 * (group >> 6) + 3 * (group & 7) + ((row & 7) >> 1)
-        slot = ((group >> 3) & 7) * 45 + jnp.where((slot < 45) & ((row & 7) < 6), slot, 0)
+        slot = jnp.where(((row >> 8) & 1) == 1, 2, (row & 3) >> 1)
+        slot = 24 * (row >> 9) + 3 * ((row >> 2) & 7) + slot
+        slot = ((row >> 5) & 7) * 45 + jnp.where(slot < 45, slot, 0)
         pick = jnp.where(col == slot, 1.0, 0.0).astype(jnp.bfloat16)
         dims = (((1,), (1,)), ((), ()))
         hi = lax.dot_general(pick, half, dims, preferred_element_type=jnp.float32)
@@ -62,7 +63,7 @@
 
 
 def basis_block(b, tab_ref, hi_ref, lo_ref):
-    start = pl.multiple_of(b * BLK, BLK)
+    start = b * BLK
     u = tab_ref[pl.ds(start, BLK), :]
     lane = lax.broadcasted_iota(jnp.int32, (BLK, 128), 1).astype(jnp.float32)
     part = (lax.broadcasted_iota(jnp.int32, (BLK, 128), 0) & 1).astype(jnp.float32)
@@ -71,6 +72,8 @@
         wave = jnp.where(odd == float(h), u, float(DEG - 1) - u)
         c, s = cos_sin(wave * lane + 360.0 * part)
         weight = jnp.where(wave == 0.0, 1.0, 2.0)
+        if b % 8 >= 4:
+            weight = jnp.where((lax.broadcasted_iota(jnp.int32, (BLK, 128), 0) >> 1) & 1 == h, weight, 0.0)
         c, s = c * weight, s * weight
         cj, sj = cos_sin(wave * 128.0)
         for j in range(6):
@@ -116,22 +119,22 @@
         out[:, :, :, 128 * t : 128 * t + 128] = rows[t].astype(jnp.bfloat16).reshape(16, 3, 4, 128)
 
 
-def legendre_sums(waves, table_ref, coef_ref, sums_ref, rows_ref, out_ref):
+def legendre_sums(waves, table_ref, coef_ref, sums_ref, rows_ref):
     table = table_ref[...].reshape(256, 768)
-    row = lax.broadcasted_iota(jnp.int32, (768, 168), 0)
-    col = lax.broadcasted_iota(jnp.int32, (768, 168), 1)
-    for s in range(3):
-        coefs = coef_ref[..., 168 * s : 168 * s + 168].reshape(768, 168)
-        u = waves[s]
-        odd = lax.rem(u, 2)
-        first = DEG - u
-        for h in range(2):
-            low = jnp.where(odd == h, 0, first)
-            high = jnp.where(odd == h, first, DEG + 1)
-            kept = jnp.where((row >= low) & (row < high), coefs, jnp.zeros((), coefs.dtype))
-            sums = jnp.dot(table, kept, preferred_element_type=jnp.float32)
-            for e in range(2):
-                sums_ref[6 * h + 2 * s + e, :, 0:CH] = sums[:, CH * e : CH * e + CH]
+    coefs = coef_ref[...].reshape(768, 512)
+    row = lax.broadcasted_iota(jnp.int32, (768, 512), 0)
+    slot = lax.broadcasted_iota(jnp.int32, (1, 512), 1)
+
+    def by_slot(values):
+        return jnp.where(slot < 168, values[0], jnp.where(slot < 336, values[1], values[2]))
+
+    for h in range(2):
+        low = by_slot([jnp.where(lax.rem(u, 2) == h, 0, DEG - u) for u in waves])
+        high = by_slot([jnp.where(lax.rem(u, 2) == h, DEG - u, DEG + 1) for u in waves])
+        kept = jnp.where((row >= low) & (row < high), coefs, jnp.zeros((), coefs.dtype))
+        sums = jnp.dot(table, kept, preferred_element_type=jnp.float32)
+        for t in range(6):
+            sums_ref[6 * h + t, :, 0:CH] = sums[:, CH * t : CH * t + CH]
     lane = lax.broadcasted_iota(jnp.int32, (8, 128), 1)
     for h in range(2):
         for s in range(3):
@@ -142,15 +145,17 @@
                     a = lats[i] if off == 0 else pltpu.roll(lats[i], 128 - off, 1)
                     b = pltpu.roll(lats[i + 1], CH - off, 1)
                     chunk = jnp.where(lane < CH - off, a, jnp.where(lane < CHUNK, b, 0.0))
-                    rows_ref[pl.ds(16 * k + 8 * h + 2 * s + e, 8, stride=128), :] = chunk
-    lanes = lax.broadcasted_iota(jnp.int32, (128, 128), 1)
-    for b in range(8):
-        x = rows_ref[128 * b : 128 * b + 128, :]
-        top = jnp.maximum(jnp.max(jnp.abs(x), axis=1, keepdims=True), 1e-37)
-        level = jnp.ceil(8.0 * jnp.log2(top) + 0.01)
-        x = jnp.floor(x * jnp.exp2(level * -0.125) * 32767.0 + 0.5)
-        x = jnp.where(lanes == CHUNK, level, x)
-        out_ref[8 * b : 8 * b + 8] = x.astype(jnp.int32).astype(jnp.int16).reshape(8, 16, 128)
+                    at = e + (2 * s if h == 0 else 6 if s == 2 else 8 + 2 * s)
+                    rows_ref[pl.ds(12 * k + at, 8, stride=96), :] = chunk
+
+def packed(rows_ref, source):
+    lanes = lax.broadcasted_iota(jnp.int32, (96, 128), 1)
+    x = rows_ref[pl.ds(pl.multiple_of(96 * source, 96), 96), :]
+    top = jnp.maximum(jnp.max(jnp.abs(x), axis=1, keepdims=True), 1e-37)
+    level = jnp.ceil(8.0 * jnp.log2(top) + 0.01)
+    x = jnp.floor(x * jnp.exp2(level * -0.125) * 32767.0 + 0.5)
+    x = jnp.where(lanes == CHUNK, level, x)
+    return x.astype(jnp.int32).astype(jnp.int16).reshape(8, 3, 4, 128)
 
 
 def kernel(pw_s, table_hbm, coef_hbm, out_ref, table_raw, coef_raw, wide_t, rows_t, wide_c, rows_c, table_in, coef_in,
@@ -196,20 +201,21 @@
     get_table.wait()
     pack_tables(table_raw, wide_t, rows_t, table_in)
 
-    tables = []
-
-    def send_tables(ds):
-        for d in ds:
-            za, yb = lax.rem(z + d, 8), lax.rem(y + d, 8)
-            tables.append(launch(copy(table_in.at[za], table_a.at[z], ts.at[0, d], tr.at[0, d], along_z[d])))
-            tables.append(launch(copy(table_in.at[8 + yb], table_b.at[y], ts.at[1, d], tr.at[1, d], along_y[d])))
+    tables = ([], [])
+
+    def send_tables(turn):
+        for half, (mine, table, peers) in enumerate(((z, table_a, along_z), (y, table_b, along_y))):
+            for d in SENDS[half][turn]:
+                to = lax.rem(mine + d, 8)
+                tables[half].append(
+                    launch(copy(table_in.at[8 * half + to], table.at[mine], ts.at[half, d], tr.at[half, d], peers[d]))
+                )
 
     def basis(b):
         basis_block(b, tab, hi, lo)
 
-    send_tables(ORDER[:2])
+    send_tables(0)
     wave_rows(pw_s, pw_v, tab)
-    rows_s[...] = jnp.zeros_like(rows_s)
 
     def chunk_here(half, mine, at, peers):
         d = lax.rem(mine - at + 8, 8)
@@ -219,45 +225,45 @@
     for s in range(4):
         for k, turn in enumerate((0, 1, 3, 2)):
             pz, py = lax.rem(z // 2 + turn, 4), lax.rem(y // 2 + turn, 4)
-            if s == 0:
-                if turn == 0:
-                    chunk_here(0, z, z + 1 - 2 * lax.rem(z, 2), along_z)
-                    chunk_here(1, y, y + 1 - 2 * lax.rem(y, 2), along_y)
-                else:
-                    for n in range(2):
-                        chunk_here(0, z, 2 * pz + n, along_z)
-                        chunk_here(1, y, 2 * py + n, along_y)
-            for way in range(2):
-                if s == 3 and (k < 2) != (way == 0):
-                    continue
-                if s > 0:
-                    for c in arriving.pop((s - 1, k, way)):
-                        c.wait_recv()
-                sign = 1 if way == 0 else 7
-                by, bz = lax.rem(y + (8 - sign) * s, 8), lax.rem(z + (8 - sign) * s, 8)
-                arriving[s, k, way] = []
-                ref_a = coef_a.at[by, pl.ds(2 * pz, 2)]
-                ref_b = coef_b.at[pl.ds(2 * py, 2), bz]
-                a = copy(ref_a, ref_a, rs.at[0, way, s, k], rr.at[0, way, s, k], along_y[sign])
-                b = copy(ref_b, ref_b, rs.at[1, way, s, k], rr.at[1, way, s, k], along_z[sign])
-                arriving[s, k, way] += [launch(a), launch(b)]
+            for half, (mine, peers) in enumerate(((z, along_z), (y, along_y))):
+                if s == 0:
+                    if turn == 0:
+                        chunk_here(half, mine, mine + 1 - 2 * lax.rem(mine, 2), peers)
+                    else:
+                        for n in range(2):
+                            chunk_here(half, mine, 2 * (py if half else pz) + n, peers)
+                for way in range(2):
+                    if s == 3 and (k < 2) != (way == 0):
+                        continue
+                    if s > 0:
+                        arriving.pop((s - 1, k, way, half)).wait_recv()
+                    sign = 1 if way == 0 else 7
+                    back = (8 - sign) * s
+                    if half == 0:
+                        ref, to = coef_a.at[lax.rem(y + back, 8), pl.ds(2 * pz, 2)], along_y[sign]
+                    else:
+                        ref, to = coef_b.at[pl.ds(2 * py, 2), lax.rem(z + back, 8)], along_z[sign]
+                    arriving[s, k, way, half] = launch(
+                        copy(ref, ref, rs.at[half, way, s, k], rr.at[half, way, s, k], to)
+                    )
             basis(4 * s + k)
-        send_tables(ORDER[2 + 2 * s : 4 + 2 * s])
-    for cs_ in arriving.values():
-        for c in cs_:
-            c.wait_recv()
+        send_tables(1 + s)
     table_a[z] = table_in[z]
     table_b[y] = table_in[8 + y]
 
     sets = ((table_a, coef_a, z, along_z), (table_b, coef_b, y, along_y))
     for half, (table, coef, mine, peers) in enumerate(sets):
-        for c in tables[half::2]:
+        for key, c in arriving.items():
+            if key[3] == half:
+                c.wait_recv()
+        for c in tables[half]:
             c.wait_recv()
         at = ma * 45 + half * 24 + mine * 3
         waves = [pw_s[jnp.minimum(at + s, 359)] for s in range(3)]
-        legendre_sums(waves, table, coef, sums_s, rows_s, send.at[half])
+        legendre_sums(waves, table, coef, sums_s, rows_s)
         for d in ORDER + (0,):
             to = lax.rem(mine + d, 8)
+            send[half, pl.ds(pl.multiple_of(8 * to, 8), 8)] = packed(rows_s, to)
 
             def step(n, _, d=d, to=to, half=half, mine=mine, peers=peers):
                 m2 = lax.rem(ma + n, 8)
@@ -275,7 +281,8 @@
         most = pl.ds(0, 63)
         copy(send.at[half, most], held.at[half, most], fs.at[half], fr.at[half], along_z[1]).wait_recv()
         for h in range(2):
-            x = held[half].astype(jnp.int32).astype(jnp.float32)[:, 8 * h : 8 * h + 8, :].reshape(512, 128)
+            own, both = (held[half, :, t].astype(jnp.int32).astype(jnp.float32).reshape(256, 128) for t in (2 * h, 1))
+            x = jnp.concatenate([own, both], axis=0)
             x = x * (jnp.exp2(x[:, CHUNK : CHUNK + 1] * 0.125) * (1.0 / 32767.0))
             high = x.astype(jnp.bfloat16)
             low = (x - high.astype(jnp.float32)).astype(jnp.bfloat16)
@@ -318,9 +325,9 @@
             pltpu.VMEM((8, 8, 3, 4, 512), bf16),
             pltpu.VMEM((8, 8, 3, 4, 512), bf16),
             pltpu.VMEM((12, 256, 128), f32),
-            pltpu.VMEM((1024, 128), f32),
-            pltpu.VMEM((2, 64, 16, 128), jnp.int16),
-            pltpu.VMEM((2, 64, 16, 128), jnp.int16),
+            pltpu.VMEM((768, 128), f32),
+            pltpu.VMEM((2, 64, 3, 4, 128), jnp.int16),
+            pltpu.VMEM((2, 64, 3, 4, 128), jnp.int16),
             dma((2,)),
             dma((2, 8)), dma((2, 8)), dma((2, 8)), dma((2, 8)),
             dma((2, 2, 4, 4)), dma((2, 2, 4, 4)), dma((2,)), dma((2,)),

time: 60.1 us -> 58.6 us (0.975)
  Pallas kernels: 57.9 us -> 56.4 us
    pallas_call x1, Pallas kernels: 57.9 us -> 56.4 us  [body(): pl.pallas_call(kernel, out_shape=jax.ShapeDtypeStruct((CHUNK, LON), f32),...]
where the time goes in v3:
time: 58.6 us; the launch traced here: 58.4 us
  Pallas kernels  56.4 us (96%)
  local copies, waits for them, and re-layouts  2 us (3%)
    pallas_call x1, Pallas kernels, body(): pl.pallas_call(kernel, out_shape=jax.ShapeDtypeStruct((CHUNK, LON), f32),...  56.4 us
    unnamed x1, local copies, waits for them, and re-layouts  2 us

profile of v3, /device:TPU:1, one launch (start us, length us, event | category | flops | bytes accessed | tf_op | source)
XLA Modules:
  0.0 58.4 jit_solution(5073614709618686012)
XLA Ops:
  0.0 56.4 %shard_map.37 = f32[105,1440]{1,0:T(8,128)} custom-call(s32[360]{0:T(512)} %pw_s.1, bf16[10,45,768]{2,1,0:T(8,128)(2,1)} %bitcast.2, bf16[12,45,168]{2,1,0:T(8,128)(2,1)} %bitcast.3), custom_call_target="tpu_custom_call" | custom-call | tf_op jit(solution)/shard_map/pallas_call | solution.py:305
  56.4 2.0 %copy.5 = f32[105,1440]{1,0:T(8,128)} copy(f32[105,1440]{1,0:T(8,128)} %shard_map.37) | data formatting | bytes 1209600

commit v4 on v3

--- a/solution.py
+++ b/solution.py
@@ -265,14 +265,17 @@
             to = lax.rem(mine + d, 8)
             send[half, pl.ds(pl.multiple_of(8 * to, 8), 8)] = packed(rows_s, to)
 
-            def step(n, _, d=d, to=to, half=half, mine=mine, peers=peers):
-                m2 = lax.rem(ma + n, 8)
+        def out(n, ds, half=half, mine=mine, peers=peers):
+            m2 = lax.rem(ma + n, 8)
+            for d in ds:
+                to = lax.rem(mine + d, 8)
                 copy(
                     send.at[half, to * 8 + m2], held.at[half, ma * 8 + mine], fs.at[half], fr.at[half], (peers[d][0], m2)
                 ).start()
-                return 0
-
-            lax.fori_loop(0 if d else 1, 8, step, 0)
+            return 0
+
+        lax.fori_loop(1, 8, lambda n, _, out=out: out(n, ORDER + (0,)), 0)
+        out(0, ORDER)
         held[half, ma * 8 + mine] = send[half, mine * 8 + ma]
 
     dims = (((0,), (0,)), ((), ()))

time: 58.6 us -> 57.2 us (0.976)
  Pallas kernels: 56.4 us -> 55 us
    pallas_call x1, Pallas kernels: 56.4 us -> 55 us  [body(): pl.pallas_call(kernel, out_shape=jax.ShapeDtypeStruct((CHUNK, LON), f32),...]
where the time goes in v4:
time: 57.2 us; the launch traced here: 57 us
  Pallas kernels  55 us (96%)
  local copies, waits for them, and re-layouts  2 us (3%)
    pallas_call x1, Pallas kernels, body(): pl.pallas_call(kernel, out_shape=jax.ShapeDtypeStruct((CHUNK, LON), f32),...  55 us
    unnamed x1, local copies, waits for them, and re-layouts  2 us

profile of v4, /device:TPU:1, one launch (start us, length us, event | category | flops | bytes accessed | tf_op | source)
XLA Modules:
  0.0 57.0 jit_solution(17770834224910474137)
XLA Ops:
  0.0 55.0 %shard_map.37 = f32[105,1440]{1,0:T(8,128)} custom-call(s32[360]{0:T(512)} %pw_s.1, bf16[10,45,768]{2,1,0:T(8,128)(2,1)} %bitcast.2, bf16[12,45,168]{2,1,0:T(8,128)(2,1)} %bitcast.3), custom_call_target="tpu_custom_call" | custom-call | tf_op jit(solution)/shard_map/pallas_call | solution.py:308
  55.0 2.0 %copy.5 = f32[105,1440]{1,0:T(8,128)} copy(f32[105,1440]{1,0:T(8,128)} %shard_map.37) | data formatting | bytes 1209600
